TPU v7x, 32 devices: a whole 2x2x4 slice. The times are simulated.
32 devices in a mesh: groups: 2 (over y), batch: 8 (over z, x), heads: 2 (over core).
Axes of the slice: x: 2, y: 2, z: 4, core: 2. Of those that a mesh axis runs over, the one named last changes fastest.
Arguments:
- storage: bfloat16 [1, 4096, 4608], P(None, ('groups', 'batch', 'heads')), parts along dimension 1, may hold values from -6 to 6
- block_table: int32 [4096], P('groups'), parts along dimension 0, may hold values from 0 to 2047, as said below
- lengths: int32 [16], P(('groups', 'batch')), parts along dimension 0, may hold values from 4 to 2048
- query: bfloat16 [16, 4, 128, 576], P(('groups', 'batch'), None, 'heads'), parts along dimension 0, may hold values from -10 to 10
Outputs:
- context: bfloat16 [16, 4, 128, 512], P(('groups', 'batch'), None, 'heads'), parts along dimension 0
There are 2 independent parts, one for each index of `groups`. A program takes and returns all parts, laid end to end along the dimension named above; each array names one. Nothing has to cross between parts.
Inputs may be any that keep to these rules, and one draw needn't show every extreme that they name: `block_table`: the entries are a permutation of 0 to 2047; entry g names block g mod 256 of sequence g // 256. Storage device k of the batch+heads order, with k = 2 b + p, holds for every batch index j exactly 16 blocks of sequences j * 1 to (j + 1) - 1, all with block numbers from p * 128 to (p + 1) * 128 - 1, in no particular order.
All inputs are finite; a program needn't handle non-finite values.
Results may differ from a plain program's by a relative error of at most 0.0031.
Values may be sent and summed in bfloat16 or wider, within the bound.
A program may use at most 64 MiB of HBM per device.

v0:
```python
import functools
import math

import jax
import jax.numpy as jnp
from jax import lax
from jax.experimental import pallas as pl
from jax.experimental.pallas import tpu as pltpu
from jax.sharding import PartitionSpec as P

MESH = pl.DeviceIdType.MESH
NT = (((1,), (1,)), ((), ()))
LATENT = 512
ROPE = 64
HEAD_NOPE = 128
SEQ_DEV = 1
MAXLEN = 2048
BLK = 8
QTOK = 4


def partial_softmax(query_rows, key_rows, first_place, limits, score_scale):
    scores = (
        jnp.einsum("src,stc->srt", query_rows, key_rows, preferred_element_type=jnp.float32)
        * score_scale
    )
    places = first_place + jnp.arange(key_rows.shape[1], dtype=jnp.int32)
    visible = places[None, None, :] <= limits[:, :, None]
    masked = jnp.where(visible, scores, -1e30)
    highest = jnp.max(masked, axis=2)
    raised = jnp.where(visible, jnp.exp(masked - highest[:, :, None]), 0.0)
    totals = jnp.sum(raised, axis=2)
    mixed = jnp.einsum(
        "srt,stc->src",
        raised.astype(jnp.bfloat16),
        key_rows[:, :, :LATENT],
        preferred_element_type=jnp.float32,
    )
    return (highest, totals, mixed)


def plain_local(storage, block_table, lengths, query):
    batch_count = lax.axis_size("batch")
    head_groups = lax.axis_size("heads")
    my_batch = lax.axis_index("batch")
    my_half = lax.axis_index("heads")
    slot_count = storage.shape[1]
    per_peer = slot_count // batch_count
    block_count = MAXLEN // BLK
    half_blocks = block_count // head_groups
    width = LATENT + ROPE
    zero_index = jnp.zeros((), jnp.int32)
    table_grid = block_table.reshape(batch_count, head_groups, slot_count)
    own_table = lax.dynamic_slice(
        table_grid, (my_batch, my_half, zero_index), (1, 1, slot_count)
    ).reshape(slot_count)
    owner = own_table // block_count // SEQ_DEV
    owner_table = (owner[:, None] == jnp.arange(batch_count, dtype=jnp.int32)[None, :]).astype(
        jnp.int32
    )
    rank = jnp.sum(owner_table * (jnp.cumsum(owner_table, axis=0) - 1), axis=1)
    send_place = owner * per_peer + rank
    order = (
        jnp.zeros((slot_count,), jnp.int32)
        .at[send_place]
        .set(jnp.arange(slot_count, dtype=jnp.int32))
    )
    outgoing = jnp.take(storage, order, axis=1)
    received = lax.all_to_all(outgoing, "batch", split_axis=1, concat_axis=1, tiled=True)
    sender_table = lax.dynamic_slice(
        table_grid, (zero_index, my_half, zero_index), (batch_count, 1, slot_count)
    ).reshape(batch_count, slot_count)
    sequence_ids = sender_table // block_count
    arrivals = sequence_ids // SEQ_DEV == my_batch
    arrive_place = (
        jnp.arange(batch_count, dtype=jnp.int32)[:, None] * per_peer
        + jnp.cumsum(arrivals.astype(jnp.int32), axis=1)
        - 1
    )
    target = (
        (sequence_ids - my_batch * SEQ_DEV) * half_blocks
        + sender_table % block_count
        - my_half * half_blocks
    )
    target = jnp.where(arrivals, target, slot_count)
    source = (
        jnp.zeros((slot_count,), jnp.int32)
        .at[target.reshape(-1)]
        .set(arrive_place.reshape(-1), mode="drop")
    )
    serving = jnp.take(received, source, axis=1)
    half_length = half_blocks * BLK
    seq_count = query.shape[0]
    local_keys = serving[0].reshape(seq_count, half_length * width)
    score_scale = 1.0 / math.sqrt(HEAD_NOPE + ROPE)
    every_query = lax.all_gather(query, "heads", axis=2, tiled=True)
    all_heads = every_query.shape[2]
    row_count = QTOK * all_heads
    query_rows = every_query.reshape(seq_count, row_count, width)
    draft = jnp.arange(row_count, dtype=jnp.int32) // all_heads
    limits = lengths[:, None] - QTOK + draft[None, :]
    key_rows = local_keys.reshape(seq_count, half_length, width)
    highest, totals, mixed = partial_softmax(
        query_rows, key_rows, my_half * half_length, limits, score_scale
    )
    shaped = (
        highest.reshape(1, seq_count, QTOK, all_heads),
        totals.reshape(1, seq_count, QTOK, all_heads),
        mixed.reshape(1, seq_count, QTOK, all_heads, LATENT),
    )
    pieces = (
        lax.all_to_all(shaped[0], "heads", split_axis=3, concat_axis=0, tiled=True),
        lax.all_to_all(shaped[1], "heads", split_axis=3, concat_axis=0, tiled=True),
        lax.all_to_all(shaped[2], "heads", split_axis=3, concat_axis=0, tiled=True),
    )
    overall = jnp.max(pieces[0], axis=0)
    factor = jnp.exp(pieces[0] - overall[None])
    totals = jnp.sum(pieces[1] * factor, axis=0)
    mixed = jnp.sum(pieces[2] * factor[..., None], axis=0)
    context = (mixed / totals[..., None]).astype(jnp.bfloat16)
    return context


def fused_kernel(
    batch_count, table_ref, length_ref, storage_ref, query_ref, out_ref,
    tabled, lengthy, stored, asked, outgoing, keys, query_even, query_odd,
    load_sem, fetch_sem, send_sem, recv_sem, pass_sem, take_sem,
):
    slot_count = stored.shape[0]
    per_peer = slot_count // batch_count
    block_count = MAXLEN // BLK
    width = LATENT + ROPE
    wide = query_even.shape[1]
    me = lax.axis_index("batch")
    half = lax.axis_index("heads")
    sibling = 1 - half

    def partner(step):
        other = me
        bit = 1
        while bit < batch_count:
            if step & bit:
                other = other + bit * (1 - 2 * ((me // bit) % 2))
            bit *= 2
        return other

    pieces = BLK // 2
    span = 2 * width

    def columns(piece):
        return pl.ds(piece * span, span)

    load_table = pltpu.make_async_copy(table_ref, tabled, load_sem.at[0])
    load_query = pltpu.make_async_copy(query_ref, asked, load_sem.at[1])
    load_length = pltpu.make_async_copy(length_ref, lengthy, load_sem.at[2])
    fetches = [
        pltpu.make_async_copy(
            storage_ref.at[:, columns(piece)], stored.at[:, columns(piece)], fetch_sem.at[piece]
        )
        for piece in range(pieces)
    ]
    load_table.start()
    for fetch in fetches:
        fetch.start()
    barrier = pltpu.get_barrier_semaphore()
    for step in range(1, batch_count):
        pl.semaphore_signal(
            barrier, inc=1, device_id={"batch": partner(step)}, device_id_type=MESH
        )
    pl.semaphore_signal(barrier, inc=1, device_id={"heads": sibling}, device_id_type=MESH)

    load_query.start()
    load_length.start()

    load_table.wait()
    table = tabled[...]
    device_count = table.shape[0]
    row_ids = lax.broadcasted_iota(jnp.int32, table.shape, 0)
    square = (slot_count, slot_count)
    down = lax.broadcasted_iota(jnp.int32, square, 0)
    across = lax.broadcasted_iota(jnp.int32, square, 1)
    earlier = (down < across).astype(jnp.float32).astype(jnp.bfloat16)
    own = jnp.sum(jnp.where(row_ids == 2 * me + half, table, 0), axis=0, keepdims=True)
    owner = own // block_count
    belongs = (row_ids == owner).astype(jnp.float32)
    counts = jnp.dot(belongs.astype(jnp.bfloat16), earlier, preferred_element_type=jnp.float32)
    rank = jnp.sum(belongs * counts, axis=0, keepdims=True).astype(jnp.int32)
    place = owner * per_peer + rank
    order = (down == place).astype(jnp.float32).astype(jnp.bfloat16)

    def group(piece):
        fetches[piece].wait()
        outgoing[:, columns(piece)] = jnp.dot(
            order, stored[:, columns(piece)], preferred_element_type=jnp.float32
        ).astype(jnp.bfloat16)

    def rows(index):
        return pl.ds(pl.multiple_of(index * per_peer, per_peer), per_peer)

    def send(step, piece):
        other = partner(step)
        return pltpu.make_async_remote_copy(
            src_ref=outgoing.at[rows(other), columns(piece)],
            dst_ref=keys.at[0, rows(me), columns(piece)],
            send_sem=send_sem.at[piece, step],
            recv_sem=recv_sem.at[piece, step],
            device_id={"batch": other},
            device_id_type=MESH,
        )

    def arrival(step, piece):
        other = partner(step)
        return pltpu.make_async_remote_copy(
            src_ref=outgoing.at[rows(other), columns(piece)],
            dst_ref=keys.at[0, rows(other), columns(piece)],
            send_sem=send_sem.at[piece, step],
            recv_sem=recv_sem.at[piece, step],
            device_id={"batch": other},
            device_id_type=MESH,
        )

    def hand_over(step, piece):
        other = partner(step)
        source = outgoing if step == 0 else keys.at[0]
        return pltpu.make_async_remote_copy(
            src_ref=source.at[rows(other), columns(piece)],
            dst_ref=keys.at[1, rows(other), columns(piece)],
            send_sem=pass_sem.at[piece, step],
            recv_sem=take_sem.at[piece, step],
            device_id={"heads": sibling},
            device_id_type=MESH,
        )

    steps = list(range(1, batch_count))

    def send_all(piece):
        for step in steps:
            send(step, piece).start()

    group(0)
    pl.semaphore_wait(barrier, batch_count)
    send_all(0)
    for piece in range(1, pieces):
        group(piece)
        if piece > 1:
            send_all(piece - 1)
    mine = table // block_count == me
    marks = mine.astype(jnp.float32)
    ranks = jnp.dot(
        marks.astype(jnp.bfloat16), earlier, preferred_element_type=jnp.float32
    ).astype(jnp.int32)
    targets = jnp.where(mine, (row_ids // 2) * per_peer + ranks, -1)
    blocks = (table % block_count).astype(jnp.float32).astype(jnp.bfloat16)
    by_half = [jnp.zeros((1, slot_count), jnp.float32) for _ in range(2)]
    for index in range(device_count):
        pick = (down == targets[index : index + 1]).astype(jnp.float32).astype(jnp.bfloat16)
        by_half[index % 2] += lax.dot_general(
            blocks[index : index + 1], pick, NT, preferred_element_type=jnp.float32
        )
    first_half = half == 0
    numbers = jnp.concatenate(
        [
            jnp.where(first_half, by_half[0], by_half[1]),
            jnp.where(first_half, by_half[1], by_half[0]),
        ],
        axis=1,
    ).astype(jnp.int32)
    for piece in range(pieces):
        hand_over(0, piece).start()
    keep = pltpu.make_async_copy(outgoing.at[rows(me)], keys.at[0, rows(me)], load_sem.at[3])
    keep.start()
    send_all(pieces - 1)

    row_count = asked.shape[0]
    heads = row_count // QTOK
    draft = lax.broadcasted_iota(jnp.int32, (row_count, 1), 0) // heads
    load_length.wait()
    limits = lengthy[0] - QTOK + draft

    load_query.wait()
    space = wide - width
    query_even[:, :width] = asked[...]
    query_even[:, width:] = jnp.zeros((row_count, space), jnp.bfloat16)
    query_odd[:, space:] = asked[...]
    query_odd[:, :space] = jnp.zeros((row_count, space), jnp.bfloat16)

    keep.wait()
    factor = math.log2(math.e) / math.sqrt(HEAD_NOPE + ROPE)
    both = 2 * slot_count
    shifted = width // 128 * 128
    peak = jnp.full((row_count, 1), -1e30, jnp.float32)
    totals = jnp.zeros((row_count, both), jnp.float32)
    mixed_even = jnp.zeros((row_count, LATENT), jnp.float32)
    mixed_odd = jnp.zeros((row_count, wide), jnp.float32)
    for piece in range(pieces):
        for step in steps:
            arrival(step, piece).wait_recv()
            hand_over(step, piece).start()
        for step in [0] + steps:
            hand_over(step, piece).wait_recv()
        base = piece * span
        parts = [
            keys[:, :, low : low + wide].reshape(both, wide) for low in (base, base + shifted)
        ]
        scores = []
        for i, queries in enumerate((query_even, query_odd)):
            dots = lax.dot_general(queries[...], parts[i], NT, preferred_element_type=jnp.float32)
            visible = numbers * BLK + (2 * piece + i) <= limits
            scores.append(jnp.where(visible, dots, -1e30))
        higher = jnp.max(jnp.maximum(scores[0], scores[1]), axis=1, keepdims=True)
        higher = jnp.maximum(peak, higher)
        shrink = jnp.exp2((peak - higher) * factor)
        peak = higher
        raised = [jnp.exp2((one - peak) * factor) for one in scores]
        totals = totals * shrink + (raised[0] + raised[1])
        mixed_even = mixed_even * shrink + jnp.dot(
            raised[0].astype(jnp.bfloat16), parts[0][:, :LATENT], preferred_element_type=jnp.float32
        )
        mixed_odd = mixed_odd * shrink + jnp.dot(
            raised[1].astype(jnp.bfloat16), parts[1], preferred_element_type=jnp.float32
        )
    total = jnp.sum(totals, axis=1, keepdims=True)
    mixed = mixed_even + mixed_odd[:, space : space + LATENT]
    out_ref[...] = (mixed / total).astype(out_ref.dtype)
    for piece in range(pieces):
        for step in steps:
            send(step, piece).wait_send()
        for step in [0] + steps:
            hand_over(step, piece).wait_send()


def local(storage, block_table, lengths, query):
    batch_count = lax.axis_size("batch")
    slot_count = storage.shape[1]
    per_peer = slot_count // batch_count
    whole = batch_count & (batch_count - 1) == 0 and query.shape[0] == SEQ_DEV
    if per_peer % 16 or slot_count % 128 or not whole:
        return plain_local(storage, block_table, lengths, query)
    width = LATENT + ROPE
    heads = query.shape[2]
    row_count = QTOK * heads
    wide = -(-width // 128) * 128
    vmem = pl.BlockSpec(memory_space=pltpu.VMEM)
    anywhere = pl.BlockSpec(memory_space=pltpu.HBM)
    context = pl.pallas_call(
        functools.partial(fused_kernel, batch_count),
        out_shape=jax.ShapeDtypeStruct((row_count, LATENT), jnp.bfloat16),
        in_specs=[anywhere] * 4,
        out_specs=vmem,
        scratch_shapes=[
            pltpu.VMEM((block_table.shape[0] // slot_count, slot_count), jnp.int32),
            pltpu.SMEM(lengths.shape, jnp.int32),
            pltpu.VMEM((slot_count, BLK * width), jnp.bfloat16),
            pltpu.VMEM((row_count, width), jnp.bfloat16),
            pltpu.VMEM((slot_count, BLK * width), jnp.bfloat16),
            pltpu.VMEM((2, slot_count, BLK * width), jnp.bfloat16),
            pltpu.VMEM((row_count, wide), jnp.bfloat16),
            pltpu.VMEM((row_count, wide), jnp.bfloat16),
            pltpu.SemaphoreType.DMA((4,)),
            pltpu.SemaphoreType.DMA((BLK // 2,)),
            pltpu.SemaphoreType.DMA((BLK // 2, batch_count)),
            pltpu.SemaphoreType.DMA((BLK // 2, batch_count)),
            pltpu.SemaphoreType.DMA((BLK // 2, batch_count)),
            pltpu.SemaphoreType.DMA((BLK // 2, batch_count)),
        ],
        compiler_params=pltpu.CompilerParams(collective_id=0, has_side_effects=True, vmem_limit_bytes=54800 * 1024),
    )(
        block_table.reshape(-1, slot_count),
        lengths,
        storage[0],
        query.reshape(row_count, width),
    )
    return context.reshape(1, QTOK, heads, LATENT)


def solution(mesh):
    in_specs = (
        P(None, ("groups", "batch", "heads"), None),
        P("groups"),
        P(("groups", "batch")),
        P(("groups", "batch"), None, "heads", None),
    )
    out_specs = P(("groups", "batch"), None, "heads", None)
    return jax.shard_map(local, mesh=mesh, in_specs=in_specs, out_specs=out_specs, check_vma=False)
```

profile of v0, /device:TPU:1, one launch (start us, length us, event | category | flops | bytes accessed | tf_op | source)
XLA Modules:
  0.0 36.6 jit_solution(11268339542790255241)
XLA Ops:
  0.7 0.0 copy-start
  0.7 0.7 %copy-done = s32[2048]{0:T(1024)S(1)} copy-done((s32[2048]{0:T(1024)S(1)}, s32[2048]{0:T(1024)}, u32[]{:S(2)}) %copy-start) | copy-done | bytes 8216
  1.4 34.5 %shard_map.46 = bf16[256,512]{1,0:T(8,128)(2,1)S(1)} custom-call(s32[16,128]{1,0:T(8,128)S(1)} %bitcast.5, s32[1]{0:T(128)S(6)} %copy.6.length_ref, bf16[128,4608]{1,0:T(8,128)(2,1)} %bitcast.6, bf16[256,576]{1,0:T(8,128)(2,1)} %bitcast.7), custom_call_target="tpu_custom_call" | custom-call | tf_op jit(solution)/shard_map/pallas_call | solution.py:345
  35.9 0.7 %copy.7 = bf16[1,4,64,512]{3,2,1,0:T(8,128)(2,1)} copy(bf16[1,4,64,512]{3,2,1,0:T(8,128)(2,1)S(1)} %bitcast.4) | data formatting | bytes 524288
Async XLA Ops:
  0.7 0.7 %copy-start = (s32[2048]{0:T(1024)S(1)}, s32[2048]{0:T(1024)}, u32[]{:S(2)}) copy-start(s32[2048]{0:T(1024)} %param.5) | copy-start | bytes 24580
where the time goes:
time: 36.8 us; the launch traced here: 36.6 us
  Pallas kernels  34.5 us (94%)
  local copies, waits for them, and re-layouts  1.4 us (4%)
  between operations  0.67 us (2%)
    pallas_call x1, Pallas kernels, local(): pl.pallas_call(functools.partial(fused_kernel, batch_count), out_shape=ja...  34.5 us
    unnamed x3, local copies, waits for them, and re-layouts  1.4 us

commit v1 on v0

v1 whole, which is shorter than its diff:
```python
import functools
import math

import jax
import jax.numpy as jnp
from jax import lax
from jax.experimental import pallas as pl
from jax.experimental.pallas import tpu as pltpu
from jax.sharding import PartitionSpec as P

MESH = pl.DeviceIdType.MESH
NT = (((1,), (1,)), ((), ()))
LATENT = 512
ROPE = 64
HEAD_NOPE = 128
SEQ_DEV = 1
MAXLEN = 2048
BLK = 8
QTOK = 4
AHEAD = 1


def partial_softmax(query_rows, key_rows, first_place, limits, score_scale):
    scores = (
        jnp.einsum("src,stc->srt", query_rows, key_rows, preferred_element_type=jnp.float32)
        * score_scale
    )
    places = first_place + jnp.arange(key_rows.shape[1], dtype=jnp.int32)
    visible = places[None, None, :] <= limits[:, :, None]
    masked = jnp.where(visible, scores, -1e30)
    highest = jnp.max(masked, axis=2)
    raised = jnp.where(visible, jnp.exp(masked - highest[:, :, None]), 0.0)
    totals = jnp.sum(raised, axis=2)
    mixed = jnp.einsum(
        "srt,stc->src",
        raised.astype(jnp.bfloat16),
        key_rows[:, :, :LATENT],
        preferred_element_type=jnp.float32,
    )
    return (highest, totals, mixed)


def plain_local(storage, block_table, lengths, query):
    batch_count = lax.axis_size("batch")
    head_groups = lax.axis_size("heads")
    my_batch = lax.axis_index("batch")
    my_half = lax.axis_index("heads")
    slot_count = storage.shape[1]
    per_peer = slot_count // batch_count
    block_count = MAXLEN // BLK
    half_blocks = block_count // head_groups
    width = LATENT + ROPE
    zero_index = jnp.zeros((), jnp.int32)
    table_grid = block_table.reshape(batch_count, head_groups, slot_count)
    own_table = lax.dynamic_slice(
        table_grid, (my_batch, my_half, zero_index), (1, 1, slot_count)
    ).reshape(slot_count)
    owner = own_table // block_count // SEQ_DEV
    owner_table = (owner[:, None] == jnp.arange(batch_count, dtype=jnp.int32)[None, :]).astype(
        jnp.int32
    )
    rank = jnp.sum(owner_table * (jnp.cumsum(owner_table, axis=0) - 1), axis=1)
    send_place = owner * per_peer + rank
    order = (
        jnp.zeros((slot_count,), jnp.int32)
        .at[send_place]
        .set(jnp.arange(slot_count, dtype=jnp.int32))
    )
    outgoing = jnp.take(storage, order, axis=1)
    received = lax.all_to_all(outgoing, "batch", split_axis=1, concat_axis=1, tiled=True)
    sender_table = lax.dynamic_slice(
        table_grid, (zero_index, my_half, zero_index), (batch_count, 1, slot_count)
    ).reshape(batch_count, slot_count)
    sequence_ids = sender_table // block_count
    arrivals = sequence_ids // SEQ_DEV == my_batch
    arrive_place = (
        jnp.arange(batch_count, dtype=jnp.int32)[:, None] * per_peer
        + jnp.cumsum(arrivals.astype(jnp.int32), axis=1)
        - 1
    )
    target = (
        (sequence_ids - my_batch * SEQ_DEV) * half_blocks
        + sender_table % block_count
        - my_half * half_blocks
    )
    target = jnp.where(arrivals, target, slot_count)
    source = (
        jnp.zeros((slot_count,), jnp.int32)
        .at[target.reshape(-1)]
        .set(arrive_place.reshape(-1), mode="drop")
    )
    serving = jnp.take(received, source, axis=1)
    half_length = half_blocks * BLK
    seq_count = query.shape[0]
    local_keys = serving[0].reshape(seq_count, half_length * width)
    score_scale = 1.0 / math.sqrt(HEAD_NOPE + ROPE)
    every_query = lax.all_gather(query, "heads", axis=2, tiled=True)
    all_heads = every_query.shape[2]
    row_count = QTOK * all_heads
    query_rows = every_query.reshape(seq_count, row_count, width)
    draft = jnp.arange(row_count, dtype=jnp.int32) // all_heads
    limits = lengths[:, None] - QTOK + draft[None, :]
    key_rows = local_keys.reshape(seq_count, half_length, width)
    highest, totals, mixed = partial_softmax(
        query_rows, key_rows, my_half * half_length, limits, score_scale
    )
    shaped = (
        highest.reshape(1, seq_count, QTOK, all_heads),
        totals.reshape(1, seq_count, QTOK, all_heads),
        mixed.reshape(1, seq_count, QTOK, all_heads, LATENT),
    )
    pieces = (
        lax.all_to_all(shaped[0], "heads", split_axis=3, concat_axis=0, tiled=True),
        lax.all_to_all(shaped[1], "heads", split_axis=3, concat_axis=0, tiled=True),
        lax.all_to_all(shaped[2], "heads", split_axis=3, concat_axis=0, tiled=True),
    )
    overall = jnp.max(pieces[0], axis=0)
    factor = jnp.exp(pieces[0] - overall[None])
    totals = jnp.sum(pieces[1] * factor, axis=0)
    mixed = jnp.sum(pieces[2] * factor[..., None], axis=0)
    context = (mixed / totals[..., None]).astype(jnp.bfloat16)
    return context


def send_orders(batch_count):
    whole = list(range(1, batch_count))
    if batch_count != 8:
        return [whole] * 4, [[0] + whole] * 4
    sends = [
        [1, 2, 3, 4, 5, 6, 7],
        [6, 7, 4, 5, 2, 3, 1],
        [6, 4, 5, 7, 2, 3, 1],
        [6, 7, 2, 3, 4, 5, 1],
    ]
    uses = [
        [0, 1, 2, 3, 4, 6, 5, 7],
        [0, 1, 6, 2, 3, 7, 4, 5],
        [0, 1, 6, 7, 4, 2, 5, 3],
        [0, 1, 2, 3, 4, 5, 6, 7],
    ]
    return sends, uses


def fused_kernel(
    batch_count, table_ref, length_ref, storage_ref, query_ref, out_ref,
    tabled, lengthy, stored, asked, outgoing, keys, queries, places, mixed,
    load_sem, fetch_sem, send_sem, recv_sem, pass_sem, take_sem, ready_sem,
):
    slot_count = stored.shape[0]
    per_peer = slot_count // batch_count
    block_count = MAXLEN // BLK
    width = LATENT + ROPE
    span = 2 * width
    pieces = BLK // 2
    me = lax.axis_index("batch")
    half = lax.axis_index("heads")
    sibling = 1 - half
    depth = me // 2
    deep = batch_count // 2
    left = depth == deep // 2 - 1
    right = depth == deep // 2
    middle = left | right
    across = batch_count - 2
    sends, uses = send_orders(batch_count)
    kind = jnp.where(left, 1, jnp.where(right, 2, jnp.where(depth < deep // 2, 0, 3)))

    def flip(step):
        other = me
        bit = 1
        while bit < batch_count:
            other = other + bit * (1 - 2 * ((me // bit) % 2)) * ((step // bit) % 2)
            bit *= 2
        return other

    def chosen(table, place):
        picked = table[3][place]
        for index in range(3):
            picked = jnp.where(kind == index, table[index][place], picked)
        return picked

    def columns(piece):
        return pl.ds(piece * span, span)

    def rows(index):
        return pl.ds(pl.multiple_of(index * per_peer, per_peer), per_peer)

    load_table = pltpu.make_async_copy(table_ref, tabled, load_sem.at[0])
    load_query = pltpu.make_async_copy(query_ref, asked, load_sem.at[1])
    load_length = pltpu.make_async_copy(length_ref, lengthy, load_sem.at[2])
    fetches = [
        pltpu.make_async_copy(
            storage_ref.at[:, columns(piece)], stored.at[:, columns(piece)], fetch_sem.at[piece]
        )
        for piece in range(pieces)
    ]
    load_table.start()
    for fetch in fetches:
        fetch.start()

    barrier = pltpu.get_barrier_semaphore()

    def tell(other, core):
        pl.semaphore_signal(
            barrier, inc=1, device_id={"batch": other, "heads": core}, device_id_type=MESH
        )

    @pl.when(middle)
    def _():
        tell(flip(across), half)

    for spot in range(batch_count):
        if spot // 2 in (deep // 2 - 1, deep // 2):
            continue
        for core in range(2):

            @pl.when((me != spot) | (half != core))
            def _():
                tell(spot, core)

    load_query.start()
    load_length.start()

    load_table.wait()
    table = tabled[...]
    row_ids = lax.broadcasted_iota(jnp.int32, table.shape, 0)
    square = (slot_count, slot_count)
    down = lax.broadcasted_iota(jnp.int32, square, 0)
    along = lax.broadcasted_iota(jnp.int32, square, 1)
    earlier = (down < along).astype(jnp.float32).astype(jnp.bfloat16)
    own = jnp.sum(jnp.where(row_ids == 2 * me + half, table, 0), axis=0, keepdims=True)
    owner = own // block_count
    belongs = (row_ids == owner).astype(jnp.float32)
    counts = jnp.dot(belongs.astype(jnp.bfloat16), earlier, preferred_element_type=jnp.float32)
    rank = jnp.sum(belongs * counts, axis=0, keepdims=True).astype(jnp.int32)
    place = owner * per_peer + rank
    order = (down == place).astype(jnp.float32).astype(jnp.bfloat16)

    lanes = lax.broadcasted_iota(jnp.int32, (1, 2 * ROPE), 1)
    first_lanes = (lanes < ROPE).astype(jnp.float32).astype(jnp.bfloat16)
    last_lanes = (lanes >= ROPE).astype(jnp.float32).astype(jnp.bfloat16)

    def group(piece):
        fetches[piece].wait()
        base = piece * span
        moved = jnp.dot(
            order, stored[:, columns(piece)], preferred_element_type=jnp.float32
        )
        outgoing[:, base : base + LATENT] = moved[:, :LATENT].astype(jnp.bfloat16)
        outgoing[:, base + LATENT : base + 2 * LATENT] = moved[
            :, width : width + LATENT
        ].astype(jnp.bfloat16)
        outgoing[:, base + 2 * LATENT : base + span] = jnp.where(
            lanes < ROPE, moved[:, LATENT : LATENT + 2 * ROPE], moved[:, span - 2 * ROPE :]
        ).astype(jnp.bfloat16)

    def send(step, where):
        other = flip(step)
        return pltpu.make_async_remote_copy(
            src_ref=outgoing.at[rows(other), where],
            dst_ref=keys.at[half, rows(me), where],
            send_sem=send_sem.at[step],
            recv_sem=recv_sem.at[step],
            device_id={"batch": other},
            device_id_type=MESH,
        )

    everything = pl.ds(0, pieces * span)

    def arrival(step):
        other = flip(step)
        return pltpu.make_async_remote_copy(
            src_ref=outgoing.at[rows(other), everything],
            dst_ref=keys.at[half, rows(other), everything],
            send_sem=send_sem.at[step],
            recv_sem=recv_sem.at[step],
            device_id={"batch": other},
            device_id_type=MESH,
        )

    def hand_over(step, source):
        other = flip(step)
        return pltpu.make_async_remote_copy(
            src_ref=source.at[rows(other)],
            dst_ref=keys.at[half, rows(other)],
            send_sem=pass_sem.at[step],
            recv_sem=take_sem.at[step],
            device_id={"heads": sibling},
            device_id_type=MESH,
        )

    for piece in range(pieces):
        group(piece)

        @pl.when(middle)
        def _():
            if piece == 0:
                pl.semaphore_wait(barrier, 1)
            send(across, columns(piece)).start()

    @pl.when(middle)
    def _():
        pl.semaphore_wait(ready_sem, 1)

    @pl.when(jnp.logical_not(middle))
    def _():
        pl.semaphore_wait(barrier, 2 * batch_count - 1)

        @pl.when((depth == 0) | (depth == deep - 1))
        def _():
            inner = jnp.where(depth == 0, me + batch_count - 2 - deep, me - batch_count + 2 + deep)
            pl.semaphore_signal(
                ready_sem, inc=1, device_id={"batch": inner}, device_id_type=MESH
            )

        send(chosen(sends, 0), everything).start()

    for turn in range(1, batch_count - 1):
        send(chosen(sends, turn), everything).start()
    hand_over(0, outgoing).start()

    keys[half, rows(me)] = outgoing[rows(me)]

    mine = table // block_count == me
    marks = mine.astype(jnp.float32)
    ranks = jnp.dot(
        marks.astype(jnp.bfloat16), earlier, preferred_element_type=jnp.float32
    ).astype(jnp.int32)
    ranks = jnp.where(mine, ranks, -1)
    blocks = (table % block_count).astype(jnp.float32)
    lane = lax.broadcasted_iota(jnp.int32, table.shape, 1)
    spots = (lane // per_peer).astype(jnp.float32)
    for index in range(per_peer):
        number = jnp.sum(jnp.where(ranks == index, blocks, 0.0), axis=1, keepdims=True)
        spots = spots + jnp.where(lane % per_peer == index, number * BLK, 0.0)
    places[...] = spots

    row_count = asked.shape[0]
    heads = row_count // QTOK
    load_length.wait()
    limits = [(lengthy[0] - QTOK + draft).astype(jnp.float32) for draft in range(QTOK)]

    load_query.wait()
    asking = asked[...]
    queries[:, :width] = asking
    queries[:, width:] = asking[:, LATENT:]

    factor = math.log2(math.e) / math.sqrt(HEAD_NOPE + ROPE)
    peak = jnp.full((row_count, 1), -1e30, jnp.float32)
    totals = jnp.zeros((row_count, slot_count), jnp.float32)
    steps = [0] + [chosen(uses, turn) for turn in range(1, batch_count)]
    for turn in range(batch_count):
        if turn + AHEAD < batch_count:
            for ahead in range(1 if turn == 0 else turn + AHEAD, turn + AHEAD + 1):
                arrival(steps[ahead]).wait_recv()
                hand_over(steps[ahead], keys.at[half]).start()
        step = steps[turn]
        other = me if turn == 0 else flip(step)
        hand_over(step, keys.at[half]).wait_recv()
        latents = []
        ropes = []
        for core in range(2):
            for piece in range(pieces):
                base = piece * span
                pair = keys[core, rows(other), base + 2 * LATENT : base + span]
                for parity in range(2):
                    low = base + parity * LATENT
                    latents.append(keys[core, rows(other), low : low + LATENT])
                    ropes.append(pair * (last_lanes if parity else first_lanes))
        latent = jnp.concatenate(latents, axis=0)
        rope = jnp.concatenate(ropes, axis=0)
        dots = lax.dot_general(
            queries[...],
            jnp.concatenate([latent, rope], axis=1),
            NT,
            preferred_element_type=jnp.float32,
        )
        at = places[pl.ds(2 * other, 2), :]
        at = jnp.concatenate([at[0:1], at[1:2]], axis=1)
        scores = jnp.concatenate(
            [
                dots[draft * heads : (draft + 1) * heads]
                + jnp.where(at <= limits[draft], 0.0, -1e30)
                for draft in range(QTOK)
            ],
            axis=0,
        )
        higher = jnp.maximum(peak, jnp.max(scores, axis=1, keepdims=True))
        raised = jnp.exp2((scores - higher) * factor)
        sums = raised[:, :slot_count] + raised[:, slot_count:]
        fresh = jnp.dot(raised.astype(jnp.bfloat16), latent, preferred_element_type=jnp.float32)
        if turn == 0:
            totals = sums
            mixed[...] = fresh
        else:
            shrink = jnp.exp2((peak - higher) * factor)
            totals = totals * shrink + sums
            mixed[...] = mixed[...] * shrink + fresh
        peak = higher
    total = jnp.sum(totals, axis=1, keepdims=True)
    out_ref[...] = (mixed[...] / total).astype(out_ref.dtype)
    for step in range(1, batch_count):
        send(step, everything).wait_send()
    for step in range(batch_count):
        hand_over(step, keys.at[half]).wait_send()


def local(storage, block_table, lengths, query):
    batch_count = lax.axis_size("batch")
    slot_count = storage.shape[1]
    per_peer = slot_count // batch_count
    whole = batch_count & (batch_count - 1) == 0 and query.shape[0] == SEQ_DEV
    whole = whole and batch_count >= 8 and lax.axis_size("heads") == 2
    if per_peer % 16 or slot_count != 128 or BLK * per_peer != slot_count or not whole:
        return plain_local(storage, block_table, lengths, query)
    width = LATENT + ROPE
    heads = query.shape[2]
    row_count = QTOK * heads
    vmem = pl.BlockSpec(memory_space=pltpu.VMEM)
    anywhere = pl.BlockSpec(memory_space=pltpu.HBM)
    context = pl.pallas_call(
        functools.partial(fused_kernel, batch_count),
        out_shape=jax.ShapeDtypeStruct((row_count, LATENT), jnp.bfloat16),
        in_specs=[anywhere] * 4,
        out_specs=vmem,
        scratch_shapes=[
            pltpu.VMEM((block_table.shape[0] // slot_count, slot_count), jnp.int32),
            pltpu.SMEM(lengths.shape, jnp.int32),
            pltpu.VMEM((slot_count, BLK * width), jnp.bfloat16),
            pltpu.VMEM((row_count, width), jnp.bfloat16),
            pltpu.VMEM((slot_count, BLK * width), jnp.bfloat16),
            pltpu.VMEM((2, slot_count, BLK * width), jnp.bfloat16),
            pltpu.VMEM((row_count, LATENT + 2 * ROPE), jnp.bfloat16),
            pltpu.VMEM((block_table.shape[0] // slot_count, slot_count), jnp.float32),
            pltpu.VMEM((row_count, LATENT), jnp.float32),
            pltpu.SemaphoreType.DMA((3,)),
            pltpu.SemaphoreType.DMA((BLK // 2,)),
            pltpu.SemaphoreType.DMA((batch_count,)),
            pltpu.SemaphoreType.DMA((batch_count,)),
            pltpu.SemaphoreType.DMA((batch_count,)),
            pltpu.SemaphoreType.DMA((batch_count,)),
            pltpu.SemaphoreType.REGULAR,
        ],
        compiler_params=pltpu.CompilerParams(collective_id=0, has_side_effects=True, vmem_limit_bytes=54800 * 1024),
    )(
        block_table.reshape(-1, slot_count),
        lengths,
        storage[0],
        query.reshape(row_count, width),
    )
    return context.reshape(1, QTOK, heads, LATENT)


def solution(mesh):
    in_specs = (
        P(None, ("groups", "batch", "heads"), None),
        P("groups"),
        P(("groups", "batch")),
        P(("groups", "batch"), None, "heads", None),
    )
    out_specs = P(("groups", "batch"), None, "heads", None)
    return jax.shard_map(local, mesh=mesh, in_specs=in_specs, out_specs=out_specs, check_vma=False)
```

time: 36.8 us -> 36 us (0.978)
  the two profiles are of different devices: /device:TPU:1 before, /device:TPU:9 now
where the time goes in v1:
time: 36 us; the launch traced here: 35.7 us
  Pallas kernels  33.7 us (94%)
  local copies, waits for them, and re-layouts  1.4 us (4%)
  between operations  0.67 us (2%)
    pallas_call x1, Pallas kernels, local(): pl.pallas_call(functools.partial(fused_kernel, batch_count), out_shape=ja...  33.7 us
    unnamed x3, local copies, waits for them, and re-layouts  1.4 us

profile of v1, /device:TPU:9, one launch (start us, length us, event | category | flops | bytes accessed | tf_op | source)
XLA Modules:
  0.0 35.7 jit_solution(6401572893420420404)
XLA Ops:
  0.7 0.0 copy-start
  0.7 0.7 %copy-done = s32[2048]{0:T(1024)S(1)} copy-done((s32[2048]{0:T(1024)S(1)}, s32[2048]{0:T(1024)}, u32[]{:S(2)}) %copy-start) | copy-done | bytes 8216
  1.4 33.7 %shard_map.46 = bf16[256,512]{1,0:T(8,128)(2,1)S(1)} custom-call(s32[16,128]{1,0:T(8,128)S(1)} %bitcast.5, s32[1]{0:T(128)S(6)} %copy.6.length_ref, bf16[128,4608]{1,0:T(8,128)(2,1)} %bitcast.6, bf16[256,576]{1,0:T(8,128)(2,1)} %bitcast.7), custom_call_target="tpu_custom_call" | custom-call | tf_op jit(solution)/shard_map/pallas_call | solution.py:420
  35.0 0.7 %copy.7 = bf16[1,4,64,512]{3,2,1,0:T(8,128)(2,1)} copy(bf16[1,4,64,512]{3,2,1,0:T(8,128)(2,1)S(1)} %bitcast.4) | data formatting | bytes 524288
Async XLA Ops:
  0.7 0.7 %copy-start = (s32[2048]{0:T(1024)S(1)}, s32[2048]{0:T(1024)}, u32[]{:S(2)}) copy-start(s32[2048]{0:T(1024)} %param.5) | copy-start | bytes 24580

commit v2 on v1

--- a/solution.py
+++ b/solution.py
@@ -17,7 +17,7 @@
 MAXLEN = 2048
 BLK = 8
 QTOK = 4
-AHEAD = 1
+AHEAD = 2
 
 
 def partial_softmax(query_rows, key_rows, first_place, limits, score_scale):
@@ -128,14 +128,14 @@
         return [whole] * 4, [[0] + whole] * 4
     sends = [
         [1, 2, 3, 4, 5, 6, 7],
-        [6, 7, 4, 5, 2, 3, 1],
-        [6, 4, 5, 7, 2, 3, 1],
+        [6, 1, 2, 3, 4, 5, 7],
+        [6, 4, 5, 2, 3, 7, 1],
         [6, 7, 2, 3, 4, 5, 1],
     ]
     uses = [
-        [0, 1, 2, 3, 4, 6, 5, 7],
-        [0, 1, 6, 2, 3, 7, 4, 5],
-        [0, 1, 6, 7, 4, 2, 5, 3],
+        [0, 1, 2, 6, 4, 7, 5, 3],
+        [0, 1, 2, 3, 6, 4, 5, 7],
+        [0, 1, 6, 2, 4, 3, 5, 7],
         [0, 1, 2, 3, 4, 5, 6, 7],
     ]
     return sends, uses
@@ -442,7 +442,7 @@
         ],
         compiler_params=pltpu.CompilerParams(collective_id=0, has_side_effects=True, vmem_limit_bytes=54800 * 1024),
     )(
-        block_table.reshape(-1, slot_count),
+        pltpu.with_memory_space_constraint(block_table.reshape(-1, slot_count), pltpu.HBM),
         lengths,
         storage[0],
         query.reshape(row_count, width),

time: 36 us -> 34.6 us (0.961)
  the two profiles are of different devices: /device:TPU:9 before, /device:TPU:0 now
where the time goes in v2:
time: 34.6 us; the launch traced here: 34.5 us
  Pallas kernels  33.1 us (96%)
  local copies, waits for them, and re-layouts  0.71 us (2%)
  between operations  0.66 us (2%)
    pallas_call x1, Pallas kernels, local(): pl.pallas_call(functools.partial(fused_kernel, batch_count), out_shape=ja...  33.1 us
    unnamed x1, local copies, waits for them, and re-layouts  0.71 us

profile of v2, /device:TPU:0, one launch (start us, length us, event | category | flops | bytes accessed | tf_op | source)
XLA Modules:
  0.0 34.5 jit_solution(4219539885229514726)
XLA Ops:
  0.7 33.1 %shard_map.46 = bf16[256,512]{1,0:T(8,128)(2,1)S(1)} custom-call(s32[16,128]{1,0:T(8,128)} %bitcast.7, s32[1]{0:T(128)S(6)} %copy.6.length_ref, bf16[128,4608]{1,0:T(8,128)(2,1)} %bitcast.5, bf16[256,576]{1,0:T(8,128)(2,1)} %bitcast.6), custom_call_target="tpu_custom_call" | custom-call | tf_op jit(solution)/shard_map/pallas_call | solution.py:420
  33.8 0.7 %copy.7 = bf16[1,4,64,512]{3,2,1,0:T(8,128)(2,1)} copy(bf16[1,4,64,512]{3,2,1,0:T(8,128)(2,1)S(1)} %bitcast.4) | data formatting | bytes 524288

commit v3 on v2

--- a/solution.py
+++ b/solution.py
@@ -17,7 +17,9 @@
 MAXLEN = 2048
 BLK = 8
 QTOK = 4
+SHARES = 1
 AHEAD = 2
+HOLDS = (3, 4)
 
 
 def partial_softmax(query_rows, key_rows, first_place, limits, score_scale):
@@ -125,18 +127,26 @@
 def send_orders(batch_count):
     whole = list(range(1, batch_count))
     if batch_count != 8:
-        return [whole] * 4, [[0] + whole] * 4
+        return [whole] * 8, [[0] + whole] * 8
     sends = [
         [1, 2, 3, 4, 5, 6, 7],
-        [6, 1, 2, 3, 4, 5, 7],
+        [1, 2, 3, 4, 5, 6, 7],
+        [6, 1, 2, 3, 7, 4, 5],
+        [6, 1, 2, 3, 7, 4, 5],
         [6, 4, 5, 2, 3, 7, 1],
-        [6, 7, 2, 3, 4, 5, 1],
+        [6, 4, 5, 2, 3, 7, 1],
+        [6, 7, 2, 3, 1, 4, 5],
+        [6, 7, 2, 3, 1, 4, 5],
     ]
     uses = [
-        [0, 1, 2, 6, 4, 7, 5, 3],
+        [0, 1, 6, 7, 4, 2, 5, 3],
+        [0, 1, 6, 7, 4, 2, 5, 3],
         [0, 1, 2, 3, 6, 4, 5, 7],
-        [0, 1, 6, 2, 4, 3, 5, 7],
-        [0, 1, 2, 3, 4, 5, 6, 7],
+        [0, 1, 2, 3, 6, 4, 7, 5],
+        [0, 1, 6, 2, 4, 3, 7, 5],
+        [0, 1, 6, 2, 4, 3, 7, 5],
+        [0, 1, 2, 3, 6, 7, 4, 5],
+        [0, 1, 2, 3, 6, 7, 4, 5],
     ]
     return sends, uses
 
@@ -162,7 +172,8 @@
     middle = left | right
     across = batch_count - 2
     sends, uses = send_orders(batch_count)
-    kind = jnp.where(left, 1, jnp.where(right, 2, jnp.where(depth < deep // 2, 0, 3)))
+    stage = jnp.where(left, 1, jnp.where(right, 2, jnp.where(depth < deep // 2, 0, 3)))
+    kind = 2 * stage + me % 2
 
     def flip(step):
         other = me
@@ -173,9 +184,10 @@
         return other
 
     def chosen(table, place):
-        picked = table[3][place]
-        for index in range(3):
-            picked = jnp.where(kind == index, table[index][place], picked)
+        picked = table[0][place]
+        for index in range(1, len(table)):
+            if table[index][place] != table[0][place]:
+                picked = jnp.where(kind == index, table[index][place], picked)
         return picked
 
     def columns(piece):
@@ -228,7 +240,7 @@
     along = lax.broadcasted_iota(jnp.int32, square, 1)
     earlier = (down < along).astype(jnp.float32).astype(jnp.bfloat16)
     own = jnp.sum(jnp.where(row_ids == 2 * me + half, table, 0), axis=0, keepdims=True)
-    owner = own // block_count
+    owner = jnp.right_shift(own, block_count.bit_length() - 1)
     belongs = (row_ids == owner).astype(jnp.float32)
     counts = jnp.dot(belongs.astype(jnp.bfloat16), earlier, preferred_element_type=jnp.float32)
     rank = jnp.sum(belongs * counts, axis=0, keepdims=True).astype(jnp.int32)
@@ -258,8 +270,8 @@
         return pltpu.make_async_remote_copy(
             src_ref=outgoing.at[rows(other), where],
             dst_ref=keys.at[half, rows(me), where],
-            send_sem=send_sem.at[step],
-            recv_sem=recv_sem.at[step],
+            send_sem=send_sem,
+            recv_sem=recv_sem.at[step - 1],
             device_id={"batch": other},
             device_id_type=MESH,
         )
@@ -271,8 +283,8 @@
         return pltpu.make_async_remote_copy(
             src_ref=outgoing.at[rows(other), everything],
             dst_ref=keys.at[half, rows(other), everything],
-            send_sem=send_sem.at[step],
-            recv_sem=recv_sem.at[step],
+            send_sem=send_sem,
+            recv_sem=recv_sem.at[step - 1],
             device_id={"batch": other},
             device_id_type=MESH,
         )
@@ -282,7 +294,7 @@
         return pltpu.make_async_remote_copy(
             src_ref=source.at[rows(other)],
             dst_ref=keys.at[half, rows(other)],
-            send_sem=pass_sem.at[step],
+            send_sem=pass_sem,
             recv_sem=take_sem.at[step],
             device_id={"heads": sibling},
             device_id_type=MESH,
@@ -314,19 +326,30 @@
 
         send(chosen(sends, 0), everything).start()
 
-    for turn in range(1, batch_count - 1):
+    for turn in range(1, batch_count - 3):
         send(chosen(sends, turn), everything).start()
+
+    held = depth == deep - 1
+
+    def send_late(late):
+        send(chosen(sends, batch_count - 3 + late), everything).start()
+
+    @pl.when(jnp.logical_not(held))
+    def _():
+        for late in range(2):
+            send_late(late)
+
     hand_over(0, outgoing).start()
 
     keys[half, rows(me)] = outgoing[rows(me)]
 
-    mine = table // block_count == me
+    mine = jnp.right_shift(table, block_count.bit_length() - 1) == me
     marks = mine.astype(jnp.float32)
     ranks = jnp.dot(
         marks.astype(jnp.bfloat16), earlier, preferred_element_type=jnp.float32
     ).astype(jnp.int32)
     ranks = jnp.where(mine, ranks, -1)
-    blocks = (table % block_count).astype(jnp.float32)
+    blocks = jnp.bitwise_and(table, block_count - 1).astype(jnp.float32)
     lane = lax.broadcasted_iota(jnp.int32, table.shape, 1)
     spots = (lane // per_peer).astype(jnp.float32)
     for index in range(per_peer):
@@ -345,13 +368,20 @@
     queries[:, width:] = asking[:, LATENT:]
 
     factor = math.log2(math.e) / math.sqrt(HEAD_NOPE + ROPE)
-    peak = jnp.full((row_count, 1), -1e30, jnp.float32)
-    totals = jnp.zeros((row_count, slot_count), jnp.float32)
+    portion = row_count // SHARES
+    peaks = [jnp.full((portion, 1), -1e30, jnp.float32)] * SHARES
+    totals = [None] * SHARES
     steps = [0] + [chosen(uses, turn) for turn in range(1, batch_count)]
     for turn in range(batch_count):
         if turn + AHEAD < batch_count:
             for ahead in range(1 if turn == 0 else turn + AHEAD, turn + AHEAD + 1):
                 arrival(steps[ahead]).wait_recv()
+                if ahead in HOLDS:
+
+                    @pl.when(held)
+                    def _():
+                        send_late(HOLDS.index(ahead))
+
                 hand_over(steps[ahead], keys.at[half]).start()
         step = steps[turn]
         other = me if turn == 0 else flip(step)
@@ -368,40 +398,57 @@
                     ropes.append(pair * (last_lanes if parity else first_lanes))
         latent = jnp.concatenate(latents, axis=0)
         rope = jnp.concatenate(ropes, axis=0)
-        dots = lax.dot_general(
-            queries[...],
-            jnp.concatenate([latent, rope], axis=1),
-            NT,
-            preferred_element_type=jnp.float32,
-        )
+        whole = jnp.concatenate([latent, rope], axis=1)
         at = places[pl.ds(2 * other, 2), :]
         at = jnp.concatenate([at[0:1], at[1:2]], axis=1)
-        scores = jnp.concatenate(
-            [
-                dots[draft * heads : (draft + 1) * heads]
-                + jnp.where(at <= limits[draft], 0.0, -1e30)
-                for draft in range(QTOK)
-            ],
-            axis=0,
-        )
-        higher = jnp.maximum(peak, jnp.max(scores, axis=1, keepdims=True))
-        raised = jnp.exp2((scores - higher) * factor)
-        sums = raised[:, :slot_count] + raised[:, slot_count:]
-        fresh = jnp.dot(raised.astype(jnp.bfloat16), latent, preferred_element_type=jnp.float32)
-        if turn == 0:
-            totals = sums
-            mixed[...] = fresh
-        else:
-            shrink = jnp.exp2((peak - higher) * factor)
-            totals = totals * shrink + sums
-            mixed[...] = mixed[...] * shrink + fresh
-        peak = higher
-    total = jnp.sum(totals, axis=1, keepdims=True)
-    out_ref[...] = (mixed[...] / total).astype(out_ref.dtype)
-    for step in range(1, batch_count):
-        send(step, everything).wait_send()
-    for step in range(batch_count):
-        hand_over(step, keys.at[half]).wait_send()
+        masks = [jnp.where(at <= limits[draft], 0.0, -1e30) for draft in range(QTOK)]
+        for share in range(SHARES):
+            low, high = share * portion, (share + 1) * portion
+            dots = lax.dot_general(
+                queries[low:high], whole, NT, preferred_element_type=jnp.float32
+            )
+            scores = jnp.concatenate(
+                [
+                    dots[draft * heads - low : (draft + 1) * heads - low] + masks[draft]
+                    for draft in range(low // heads, high // heads)
+                ],
+                axis=0,
+            )
+            higher = jnp.maximum(peaks[share], jnp.max(scores, axis=1, keepdims=True))
+            raised = jnp.exp2((scores - higher) * factor)
+            sums = raised[:, :slot_count] + raised[:, slot_count:]
+            fresh = jnp.dot(
+                raised.astype(jnp.bfloat16), latent, preferred_element_type=jnp.float32
+            )
+            if turn == 0:
+                totals[share] = sums
+                mixed[low:high] = fresh
+            else:
+                shrink = jnp.exp2((peaks[share] - higher) * factor)
+                totals[share] = totals[share] * shrink + sums
+                mixed[low:high] = mixed[low:high] * shrink + fresh
+            peaks[share] = higher
+    for share in range(SHARES):
+        low, high = share * portion, (share + 1) * portion
+        inverse = 1.0 / jnp.sum(totals[share], axis=1, keepdims=True)
+        out_ref[low:high] = (mixed[low:high] * inverse).astype(out_ref.dtype)
+    others = pl.ds(0, slot_count - per_peer)
+    pltpu.make_async_remote_copy(
+        src_ref=outgoing.at[others],
+        dst_ref=keys.at[half, others],
+        send_sem=send_sem,
+        recv_sem=recv_sem.at[0],
+        device_id={"heads": sibling},
+        device_id_type=MESH,
+    ).wait_send()
+    pltpu.make_async_remote_copy(
+        src_ref=keys.at[half],
+        dst_ref=keys.at[half],
+        send_sem=pass_sem,
+        recv_sem=take_sem.at[0],
+        device_id={"heads": sibling},
+        device_id_type=MESH,
+    ).wait_send()
 
 
 def local(storage, block_table, lengths, query):
@@ -434,9 +481,9 @@
             pltpu.VMEM((row_count, LATENT), jnp.float32),
             pltpu.SemaphoreType.DMA((3,)),
             pltpu.SemaphoreType.DMA((BLK // 2,)),
-            pltpu.SemaphoreType.DMA((batch_count,)),
-            pltpu.SemaphoreType.DMA((batch_count,)),
-            pltpu.SemaphoreType.DMA((batch_count,)),
+            pltpu.SemaphoreType.DMA,
+            pltpu.SemaphoreType.DMA((batch_count - 1,)),
+            pltpu.SemaphoreType.DMA,
             pltpu.SemaphoreType.DMA((batch_count,)),
             pltpu.SemaphoreType.REGULAR,
         ],

time: 34.6 us -> 33.8 us (0.977)
  the two profiles are of different devices: /device:TPU:0 before, /device:TPU:9 now
where the time goes in v3:
time: 33.8 us; the launch traced here: 33.7 us
  Pallas kernels  32.3 us (96%)
  local copies, waits for them, and re-layouts  0.71 us (2%)
  between operations  0.66 us (2%)
    pallas_call x1, Pallas kernels, local(): pl.pallas_call(functools.partial(fused_kernel, batch_count), out_shape=ja...  32.3 us
    unnamed x1, local copies, waits for them, and re-layouts  0.71 us

profile of v3, /device:TPU:9, one launch (start us, length us, event | category | flops | bytes accessed | tf_op | source)
XLA Modules:
  0.0 33.7 jit_solution(3250429236459454237)
XLA Ops:
  0.7 32.3 %shard_map.46 = bf16[256,512]{1,0:T(8,128)(2,1)S(1)} custom-call(s32[16,128]{1,0:T(8,128)} %bitcast.7, s32[1]{0:T(128)S(6)} %copy.6.length_ref, bf16[128,4608]{1,0:T(8,128)(2,1)} %bitcast.5, bf16[256,576]{1,0:T(8,128)(2,1)} %bitcast.6), custom_call_target="tpu_custom_call" | custom-call | tf_op jit(solution)/shard_map/pallas_call | solution.py:467
  33.0 0.7 %copy.7 = bf16[1,4,64,512]{3,2,1,0:T(8,128)(2,1)} copy(bf16[1,4,64,512]{3,2,1,0:T(8,128)(2,1)S(1)} %bitcast.4) | data formatting | bytes 524288

commit v4 on v3

--- a/solution.py
+++ b/solution.py
@@ -131,20 +131,20 @@
     sends = [
         [1, 2, 3, 4, 5, 6, 7],
         [1, 2, 3, 4, 5, 6, 7],
-        [6, 1, 2, 3, 7, 4, 5],
-        [6, 1, 2, 3, 7, 4, 5],
-        [6, 4, 5, 2, 3, 7, 1],
-        [6, 4, 5, 2, 3, 7, 1],
+        [7, 1, 2, 3, 6, 4, 5],
+        [7, 1, 2, 3, 6, 4, 5],
+        [7, 4, 5, 2, 3, 6, 1],
+        [7, 4, 5, 2, 3, 6, 1],
         [6, 7, 2, 3, 1, 4, 5],
         [6, 7, 2, 3, 1, 4, 5],
     ]
     uses = [
         [0, 1, 6, 7, 4, 2, 5, 3],
         [0, 1, 6, 7, 4, 2, 5, 3],
-        [0, 1, 2, 3, 6, 4, 5, 7],
-        [0, 1, 2, 3, 6, 4, 7, 5],
-        [0, 1, 6, 2, 4, 3, 7, 5],
-        [0, 1, 6, 2, 4, 3, 7, 5],
+        [0, 1, 2, 3, 7, 4, 5, 6],
+        [0, 1, 2, 3, 7, 4, 6, 5],
+        [0, 1, 7, 2, 4, 3, 6, 5],
+        [0, 1, 7, 2, 4, 3, 6, 5],
         [0, 1, 2, 3, 6, 7, 4, 5],
         [0, 1, 2, 3, 6, 7, 4, 5],
     ]
@@ -154,7 +154,7 @@
 def fused_kernel(
     batch_count, table_ref, length_ref, storage_ref, query_ref, out_ref,
     tabled, lengthy, stored, asked, outgoing, keys, queries, places, mixed,
-    load_sem, fetch_sem, send_sem, recv_sem, pass_sem, take_sem, ready_sem,
+    load_sem, fetch_sem, send_sem, recv_sem, pass_sem, take_sem, ready_sem, ahead_of,
 ):
     slot_count = stored.shape[0]
     per_peer = slot_count // batch_count
@@ -170,7 +170,7 @@
     left = depth == deep // 2 - 1
     right = depth == deep // 2
     middle = left | right
-    across = batch_count - 2
+    across = batch_count - 1
     sends, uses = send_orders(batch_count)
     stage = jnp.where(left, 1, jnp.where(right, 2, jnp.where(depth < deep // 2, 0, 3)))
     kind = 2 * stage + me % 2
@@ -251,17 +251,13 @@
     first_lanes = (lanes < ROPE).astype(jnp.float32).astype(jnp.bfloat16)
     last_lanes = (lanes >= ROPE).astype(jnp.float32).astype(jnp.bfloat16)
 
-    def group(piece):
-        fetches[piece].wait()
-        base = piece * span
-        moved = jnp.dot(
-            order, stored[:, columns(piece)], preferred_element_type=jnp.float32
-        )
-        outgoing[:, base : base + LATENT] = moved[:, :LATENT].astype(jnp.bfloat16)
-        outgoing[:, base + LATENT : base + 2 * LATENT] = moved[
+    def gather(picks, piece, target, base):
+        moved = jnp.dot(picks, stored[:, columns(piece)], preferred_element_type=jnp.float32)
+        target[:, base : base + LATENT] = moved[:, :LATENT].astype(jnp.bfloat16)
+        target[:, base + LATENT : base + 2 * LATENT] = moved[
             :, width : width + LATENT
         ].astype(jnp.bfloat16)
-        outgoing[:, base + 2 * LATENT : base + span] = jnp.where(
+        target[:, base + 2 * LATENT : base + span] = jnp.where(
             lanes < ROPE, moved[:, LATENT : LATENT + 2 * ROPE], moved[:, span - 2 * ROPE :]
         ).astype(jnp.bfloat16)
 
@@ -300,14 +296,32 @@
             device_id_type=MESH,
         )
 
-    for piece in range(pieces):
-        group(piece)
-
-        @pl.when(middle)
-        def _():
-            if piece == 0:
-                pl.semaphore_wait(barrier, 1)
-            send(across, columns(piece)).start()
+    fetches[0].wait()
+
+    @pl.when(middle)
+    def _():
+        beside = lax.broadcasted_iota(jnp.int32, (per_peer, slot_count), 0)
+        picks = beside + flip(across) * per_peer == place
+        gather(picks.astype(jnp.float32).astype(jnp.bfloat16), 0, ahead_of, 0)
+        pl.semaphore_wait(barrier, 1)
+        pltpu.make_async_remote_copy(
+            src_ref=ahead_of,
+            dst_ref=keys.at[half, rows(me), columns(0)],
+            send_sem=send_sem,
+            recv_sem=recv_sem.at[across - 1],
+            device_id={"batch": flip(across)},
+            device_id_type=MESH,
+        ).start()
+
+    for piece in list(range(1, pieces)) + [0]:
+        if piece:
+            fetches[piece].wait()
+        gather(order, piece, outgoing, piece * span)
+        if piece:
+
+            @pl.when(middle)
+            def _():
+                send(across, columns(piece)).start()
 
     @pl.when(middle)
     def _():
@@ -486,6 +500,7 @@
             pltpu.SemaphoreType.DMA,
             pltpu.SemaphoreType.DMA((batch_count,)),
             pltpu.SemaphoreType.REGULAR,
+            pltpu.VMEM((per_peer, 2 * width), jnp.bfloat16),
         ],
         compiler_params=pltpu.CompilerParams(collective_id=0, has_side_effects=True, vmem_limit_bytes=54800 * 1024),
     )(

time: 33.8 us -> 33.7 us (level)
  no operation moved by 1% of the time
where the time goes in v4:
time: 33.7 us; the launch traced here: 33.5 us
  Pallas kernels  32.1 us (95%)
  local copies, waits for them, and re-layouts  0.71 us (2%)
  between operations  0.66 us (2%)
    pallas_call x1, Pallas kernels, local(): pl.pallas_call(functools.partial(fused_kernel, batch_count), out_shape=ja...  32.1 us
    unnamed x1, local copies, waits for them, and re-layouts  0.71 us

profile of v4, /device:TPU:9, one launch (start us, length us, event | category | flops | bytes accessed | tf_op | source)
XLA Modules:
  0.0 33.5 jit_solution(10489111545941245587)
XLA Ops:
  0.7 32.1 %shard_map.46 = bf16[256,512]{1,0:T(8,128)(2,1)S(1)} custom-call(s32[16,128]{1,0:T(8,128)} %bitcast.7, s32[1]{0:T(128)S(6)} %copy.6.length_ref, bf16[128,4608]{1,0:T(8,128)(2,1)} %bitcast.5, bf16[256,576]{1,0:T(8,128)(2,1)} %bitcast.6), custom_call_target="tpu_custom_call" | custom-call | tf_op jit(solution)/shard_map/pallas_call | solution.py:481
  32.8 0.7 %copy.7 = bf16[1,4,64,512]{3,2,1,0:T(8,128)(2,1)} copy(bf16[1,4,64,512]{3,2,1,0:T(8,128)(2,1)S(1)} %bitcast.4) | data formatting | bytes 524288

commit v5 on v4

--- a/solution.py
+++ b/solution.py
@@ -141,7 +141,7 @@
     uses = [
         [0, 1, 6, 7, 4, 2, 5, 3],
         [0, 1, 6, 7, 4, 2, 5, 3],
-        [0, 1, 2, 3, 7, 4, 5, 6],
+        [0, 1, 2, 3, 7, 4, 6, 5],
         [0, 1, 2, 3, 7, 4, 6, 5],
         [0, 1, 7, 2, 4, 3, 6, 5],
         [0, 1, 7, 2, 4, 3, 6, 5],

time: 33.7 us -> 33.5 us (level); the launches traced: 33.5 us -> 32.8 us
  Pallas kernels: 32.1 us -> 31.5 us
    pallas_call x1, Pallas kernels: 32.1 us -> 31.5 us  [local(): pl.pallas_call(functools.partial(fused_kernel, batch_count), out_shape=ja...]
where the time goes in v5:
time: 33.5 us; the launch traced here: 32.8 us
  Pallas kernels  31.5 us (94%)
  local copies, waits for them, and re-layouts  0.71 us (2%)
  between operations  0.66 us (2%)
    pallas_call x1, Pallas kernels, local(): pl.pallas_call(functools.partial(fused_kernel, batch_count), out_shape=ja...  31.5 us
    unnamed x1, local copies, waits for them, and re-layouts  0.71 us

profile of v5, /device:TPU:9, one launch (start us, length us, event | category | flops | bytes accessed | tf_op | source)
XLA Modules:
  0.0 32.8 jit_solution(1151021752270595704)
XLA Ops:
  0.7 31.5 %shard_map.46 = bf16[256,512]{1,0:T(8,128)(2,1)S(1)} custom-call(s32[16,128]{1,0:T(8,128)} %bitcast.7, s32[1]{0:T(128)S(6)} %copy.6.length_ref, bf16[128,4608]{1,0:T(8,128)(2,1)} %bitcast.5, bf16[256,576]{1,0:T(8,128)(2,1)} %bitcast.6), custom_call_target="tpu_custom_call" | custom-call | tf_op jit(solution)/shard_map/pallas_call | solution.py:481
  32.1 0.7 %copy.7 = bf16[1,4,64,512]{3,2,1,0:T(8,128)(2,1)} copy(bf16[1,4,64,512]{3,2,1,0:T(8,128)(2,1)S(1)} %bitcast.4) | data formatting | bytes 524288
